TPU v7x, 32 devices: a whole 2x2x4 slice. The times are simulated.
32 devices in a mesh: row: 8 (over z, x), col: 4 (over y, core).
Axes of the slice: x: 2, y: 2, z: 4, core: 2. Of those that a mesh axis runs over, the one named last changes fastest.
Arguments:
- density_first: bfloat16 [12288, 12288], P('row', 'col'), may hold values from -0.0068359375 to 0.0068359375
- density_second: bfloat16 [12288, 12288], P('row', 'col'), may hold values from -0.0068359375 to 0.0068359375
- basis: bfloat16 [64, 4096, 896], P(('row', 'col')), may hold values from -6 to 6
- tile_list: int32 [64, 7], P(('row', 'col')), may hold values from 0 to 95, as said below
- tile_count: int32 [64], P(('row', 'col')), may hold values from 5 to 7, as said below
- point_count: int32 [64], P(('row', 'col')), may hold values from 1024 to 4096, as said below
- offsets: float32 [3, 64, 4096], P(None, ('row', 'col')), may hold values from -5 to 5
- weights: float32 [64, 4096], P(('row', 'col')), may hold values from 0.05 to 1
- atom_of_point: int32 [64, 4096], P(('row', 'col')), may hold values from 0 to 1023, as said below
Outputs:
- density: float32 [2, 64, 4096], P(None, ('row', 'col'))
- moments: float32 [2, 9, 1024], replicated
Inputs may be any that keep to these rules, and one draw needn't show every extreme that they name: `tile_list`: the 7 tile numbers of each batch are 7 consecutive numbers in some order. `tile_count`: some batch has 7. `point_count`: some batch has 4096. `atom_of_point`: the points of batch g belong to atoms (g * 16 + j) mod 1024 with j from 0 to 7.
All inputs are finite; a program needn't handle non-finite values.
Results may differ from a plain program's by a relative error of at most 0.0003.
Values may be sent and summed in bfloat16 or wider, within the bound.
A program may use at most 192 MiB of HBM per device.

v0:
```python
import jax
import jax.numpy as jnp
from jax import lax
from jax.sharding import PartitionSpec as P

TILE = 128
ATOMS = 1024


def harmonics(offsets):
    first_axis = offsets[0]
    second_axis = offsets[1]
    third_axis = offsets[2]
    radius_sq = first_axis * first_axis + second_axis * second_axis + third_axis * third_axis
    return jnp.stack(
        [
            jnp.ones_like(first_axis),
            first_axis,
            second_axis,
            third_axis,
            first_axis * second_axis,
            second_axis * third_axis,
            3.0 * third_axis * third_axis - radius_sq,
            first_axis * third_axis,
            first_axis * first_axis - second_axis * second_axis,
        ]
    )


def local(
    density_first,
    density_second,
    basis,
    tile_list,
    tile_count,
    point_count,
    offsets,
    weights,
    atom_of_point,
):
    row_count = lax.axis_size("row")
    col_count = lax.axis_size("col")
    tile_size = TILE
    local_rows = density_first.shape[0] // tile_size
    local_cols = density_first.shape[1] // tile_size
    batches_dev = tile_list.shape[0]
    run_length = tile_list.shape[1]
    points = basis.shape[1]
    row_slots = -(-run_length // row_count)
    col_slots = -(-run_length // col_count)
    my_row = lax.axis_index("row")
    my_col = lax.axis_index("col")
    own_start = jnp.min(tile_list, axis=1)
    starts = lax.all_gather(own_start, ("row", "col"), axis=0, tiled=True)
    run_end = starts[:, None] + run_length
    first_row = starts + (my_row - starts) % row_count
    row_tile = first_row[:, None] + row_count * jnp.arange(row_slots, dtype=jnp.int32)[None, :]
    row_ok = row_tile < run_end
    row_local = jnp.where(row_ok, row_tile // row_count, 0)
    first_col = starts + (my_col - starts) % col_count
    col_tile = first_col[:, None] + col_count * jnp.arange(col_slots, dtype=jnp.int32)[None, :]
    col_ok = col_tile < run_end
    col_local = jnp.where(col_ok, col_tile // col_count, 0)
    wanted = row_ok[:, :, None] & col_ok[:, None, :]

    def pack_tiles(stored):
        tile_grid = stored.reshape(local_rows, tile_size, local_cols, tile_size).transpose(
            0, 2, 1, 3
        )
        picked = tile_grid[row_local[:, :, None], col_local[:, None, :]]
        picked = jnp.where(wanted[..., None, None], picked, jnp.zeros((), stored.dtype))
        return picked.reshape(
            row_count, col_count, batches_dev, row_slots, col_slots, tile_size, tile_size
        )

    outgoing_first = pack_tiles(density_first)
    outgoing_second = pack_tiles(density_second)
    flat_shape = (row_count * col_count,) + outgoing_first.shape[2:]
    flat_first = outgoing_first.reshape(flat_shape)
    flat_second = outgoing_second.reshape(flat_shape)
    moved_first, moved_second = (
        lax.all_to_all(flat_first, ("row", "col"), split_axis=0, concat_axis=0, tiled=True),
        lax.all_to_all(flat_second, ("row", "col"), split_axis=0, concat_axis=0, tiled=True),
    )
    arrived_first = moved_first.reshape(outgoing_first.shape)
    arrived_second = moved_second.reshape(outgoing_second.shape)
    offset_in_run = tile_list - own_start[:, None]
    owner_row = tile_list % row_count
    slot_row = offset_in_run // row_count
    owner_col = tile_list % col_count
    slot_col = offset_in_run // col_count
    batch_ids = jnp.arange(batches_dev, dtype=jnp.int32)[:, None, None]

    def assemble(arrived):
        blocks = arrived[
            owner_row[:, :, None],
            owner_col[:, None, :],
            batch_ids,
            slot_row[:, :, None],
            slot_col[:, None, :],
        ]
        return blocks.transpose(0, 1, 3, 2, 4).reshape(
            batches_dev, run_length * tile_size, run_length * tile_size
        )

    col_mask = jnp.arange(run_length)[None, :] < tile_count[:, None]
    col_mask = jnp.repeat(col_mask, tile_size, axis=1).astype(jnp.bfloat16)
    masked = basis * col_mask[:, None, :]
    point_mask = (jnp.arange(points)[None, :] < point_count[:, None]).astype(jnp.float32)

    def density_of(arrived):
        block = assemble(arrived)
        product = jnp.einsum("bpi,bij->bpj", masked, block, preferred_element_type=jnp.float32)
        return jnp.sum(product * masked.astype(jnp.float32), axis=2) * point_mask

    density = jnp.stack([density_of(arrived_first), density_of(arrived_second)])
    harmonic = harmonics(offsets)
    moment_terms = density[:, None] * (weights[None, None] * harmonic[None])
    flat_terms = moment_terms.reshape(2 * 9, -1)
    one_hot = (
        atom_of_point.reshape(-1)[:, None] == jnp.arange(ATOMS, dtype=jnp.int32)[None, :]
    ).astype(jnp.float32)
    partial_value = jnp.dot(
        flat_terms, one_hot, precision=lax.Precision.HIGHEST, preferred_element_type=jnp.float32
    )
    moments = lax.psum(partial_value, ("row", "col"))
    return (density, moments.reshape(2, 9, ATOMS))


def solution(mesh):
    placed = (
        P("row", "col"),
        P("row", "col"),
        P(("row", "col"), None, None),
        P(("row", "col"), None),
        P(("row", "col")),
        P(("row", "col")),
        P(None, ("row", "col"), None),
        P(("row", "col"), None),
        P(("row", "col"), None),
    )
    return jax.shard_map(
        local,
        mesh=mesh,
        in_specs=placed,
        out_specs=(P(None, ("row", "col"), None), P()),
        check_vma=False,
    )
```

profile of v0, /device:TPU:0, one launch (start us, length us, event | category | flops | bytes accessed | tf_op | source)
XLA Modules:
  0.0 516.1 jit_solution(7729851914212681637)
XLA Ops:
  7.2 0.8 fusion.11
  8.0 0.2 dynamic-update-slice
  8.2 42.0 %all-reduce = s32[64]{0:T(128)S(1)} all-reduce(s32[64]{0:T(128)S(1)} %dynamic-update-slice), channel_id=1, replica_groups=mesh['row'=8,'col'=4] {'row','col'}, use_global_device_ids=true, to_apply=%add | all-reduce | flops 64 | bytes 512
  50.7 0.1 reshape.452
  50.8 9.8 %copy.68 = bf16[192,8,24,128]{3,2,1,0:T(8,128)(2,1)} copy(bf16[192,8,24,128]{3,1,2,0:T(8,128)(2,1)} %bitcast.60) | data formatting | bytes 18874368
  60.6 10.0 %copy.75 = bf16[12,128,24,128]{3,1,2,0:T(8,128)(2,1)} copy(bf16[12,128,24,128]{3,2,1,0:T(8,128)(2,1)} %bitcast.51) | data formatting | bytes 18874368 | tf_op jit(solution)/shard_map/reshape | solution.py:67
  70.6 9.9 %copy.67 = bf16[192,8,24,128]{3,2,1,0:T(8,128)(2,1)} copy(bf16[192,8,24,128]{3,1,2,0:T(8,128)(2,1)} %bitcast.61) | data formatting | bytes 18874368
  80.5 10.1 %copy.76 = bf16[12,128,24,128]{3,1,2,0:T(8,128)(2,1)} copy(bf16[12,128,24,128]{3,2,1,0:T(8,128)(2,1)} %bitcast.52) | data formatting | bytes 18874368 | tf_op jit(solution)/shard_map/reshape | solution.py:67
  90.6 6.8 %gather_fusion.2 = bf16[128,128,128]{2,1,0:T(8,128)(2,1)} fusion(bf16[12,24,128,128]{3,2,1,0:T(8,128)(2,1)} %bitcast.53, s32[128]{0:T(128)S(1)} %reshape.452), kind=kCustom, calls=%fused_computation.2 | custom fusion | bytes 8389632 | tf_op jit(solution)/shard_map/gather | solution.py:70
  97.4 6.7 %gather_fusion = bf16[128,128,128]{2,1,0:T(8,128)(2,1)} fusion(bf16[12,24,128,128]{3,2,1,0:T(8,128)(2,1)} %bitcast.54, s32[128]{0:T(128)S(1)} %reshape.452), kind=kCustom, calls=%fused_computation | custom fusion | bytes 8389632 | tf_op jit(solution)/shard_map/gather | solution.py:70
  104.3 0.2 compare_and_fusion
  104.5 5.2 broadcast_select_fusion.1
  109.6 97.9 %all_to_all.10 = bf16[32,2,1,2,128,128]{5,4,3,1,2,0:T(8,128)(2,1)} all-to-all(bf16[32,2,1,2,128,128]{5,4,3,1,2,0:T(8,128)(2,1)S(1)} %get-tuple-element.13), channel_id=1, replica_groups=mesh['row'=8,'col'=4] {'row','col'}, dimensions={0} | all-to-all | bytes 8388608 | tf_op jit(solution)/shard_map/all_to_all | solution.py:83
  207.5 3.8 all-to-all-start
  211.3 0.5 all-reduce.3.cloned.1.call-start
  212.2 19.9 %copy.46 = bf16[2,4096,896]{1,2,0:T(8,128)(2,1)} copy(bf16[2,4096,896]{2,1,0:T(8,128)(2,1)} %param.11) | data formatting | bytes 29360128 | tf_op args[2]
  232.6 4.2 gather_fusion.3
  236.9 4.5 copy.56
  241.4 7.4 %reshape.487 = bf16[2,896,896]{2,1,0:T(8,128)(2,1)} reshape(bf16[2,7,128,7,128]{4,3,2,1,0:T(8,128)(2,1)} %copy.56) | data formatting | bytes 6422528 | tf_op jit(solution)/shard_map/reshape | solution.py:102
  248.8 56.7 %all-to-all-done = bf16[32,2,1,2,128,128]{5,4,3,1,2,0:T(8,128)(2,1)} async-done(((bf16[32,2,1,2,128,128]{5,4,3,1,2,0:T(8,128)(2,1)}), bf16[32,2,1,2,128,128]{5,4,3,1,2,0:T(8,128)(2,1)}, u32[]{:S(2)}, u32[]{:S(2)}) %all-to-all-start) | async-done | bytes 4194336 | tf_op jit(solution)/shard_map/all_to_all | solution.py:82
  305.6 4.2 gather_fusion.1
  309.8 4.5 copy.51
  314.3 7.6 %reshape.485 = bf16[2,896,896]{2,1,0:T(8,128)(2,1)} reshape(bf16[2,7,128,7,128]{4,3,2,1,0:T(8,128)(2,1)} %copy.51) | data formatting | bytes 6422528 | tf_op jit(solution)/shard_map/reshape | solution.py:102
  321.9 23.4 %fusion.2 = f32[2,4096]{1,0:T(2,128)S(1)} fusion(bf16[2,896,896]{2,1,0:T(8,128)(2,1)S(1)} %copy-done, bf16[2,4096,896]{1,2,0:T(8,128)(2,1)} %copy.46, bf16[2,896]{1,0:T(2,128)(2,1)S(1)} %bitcast.68), kind=kOutput, calls=%fused_computation.9 | convolution fusion | flops 13190029312 | bytes 17927680 | tf_op jit(solution)/shard_map/bpi,bij->bpj/dot_general | solution.py:113
  345.3 24.4 %fusion.1 = f32[2,4096]{1,0:T(2,128)S(1)} fusion(bf16[2,896,896]{2,1,0:T(8,128)(2,1)} %reshape.485, bf16[2,4096,896]{1,2,0:T(8,128)(2,1)} %copy.46, bf16[2,896]{1,0:T(2,128)(2,1)S(1)} %bitcast.69), kind=kOutput, calls=%fused_computation.8 | convolution fusion | flops 13190029312 | bytes 17927680 | tf_op jit(solution)/shard_map/bpi,bij->bpj/dot_general | solution.py:113
  369.9 0.2 broadcast_multiply_fusion
  370.2 0.4 pad.4
  370.5 0.5 copy.69
  371.0 10.5 %fusion = f32[18,1024]{1,0:T(8,128)S(1)} fusion(f32[18,8192]{1,0:T(8,128)S(1)} %bitcast.64, s32[8192]{0:T(1024)S(1)} %bitcast.66), kind=kOutput, calls=%fused_computation.7 | convolution fusion | flops 1820327936 | bytes 696320 | tf_op jit(solution)/shard_map/dot_general | solution.py:123
  381.5 0.7 reshape.449
  382.2 125.1 %all-reduce.3.cloned.1.call-done = f32[2,9,1024]{2,1,0:T(8,128)} async-done(((f32[2,9,1024]{2,1,0:T(8,128)}), f32[2,9,1024]{2,1,0:T(8,128)}) %all-reduce.3.cloned.1.call-update) | async-done | bytes 73744 | tf_op jit(solution)/shard_map/psum | solution.py:126
  507.3 1.6 copy.59
  (47 shorter events, 1.4 us)
Async XLA Ops:
  207.5 4.3 copy-start.5
  207.5 98.0 %all-to-all-start = ((bf16[32,2,1,2,128,128]{5,4,3,1,2,0:T(8,128)(2,1)}), bf16[32,2,1,2,128,128]{5,4,3,1,2,0:T(8,128)(2,1)}, u32[]{:S(2)}, u32[]{:S(2)}) async-start(bf16[32,2,1,2,128,128]{5,4,3,1,2,0:T(8,128)(2,1)} %get-tuple-element.12), calls=%async_computation | async-start | bytes 8388608 | tf_op jit(solution)/shard_map/all_to_all | solution.py:82
  211.3 295.9 %all-reduce.3.cloned.1.call-start = ((), (), s32[]{:S(2)}) async-start(), calls=%async_computation.2 | async-start | bytes 262144 | tf_op jit(solution)/shard_map/psum | solution.py:126
  212.1 20.0 %copy-start.7 = (s32[2]{0:T(128)S(1)}, s32[2]{0:T(128)}, u32[]{:S(2)}) copy-start(s32[2]{0:T(128)} %param.13) | copy-start | bytes 28
  212.1 20.1 %copy-start.4 = (s32[2,4096]{1,0:T(2,128)S(1)}, s32[2,4096]{1,0:T(2,128)}, u32[]{:S(2)}) copy-start(s32[2,4096]{1,0:T(2,128)} %param.17) | copy-start | bytes 98308
  212.1 20.1 %copy-start.1 = (f32[3,2,4096]{2,1,0:T(2,128)S(1)}, f32[3,2,4096]{2,1,0:T(2,128)}, u32[]{:S(2)}) copy-start(f32[3,2,4096]{2,1,0:T(2,128)} %param.15) | copy-start | bytes 294916
  212.2 20.3 %copy-start.3 = (f32[2,4096]{1,0:T(2,128)S(1)}, f32[2,4096]{1,0:T(2,128)}, u32[]{:S(2)}) copy-start(f32[2,4096]{1,0:T(2,128)} %param.16) | copy-start | bytes 98308
  314.3 7.6 %copy-start = (bf16[2,896,896]{2,1,0:T(8,128)(2,1)S(1)}, bf16[2,896,896]{2,1,0:T(8,128)(2,1)}, u32[]{:S(2)}) copy-start(bf16[2,896,896]{2,1,0:T(8,128)(2,1)} %reshape.487) | copy-start | bytes 9633796
  345.3 24.5 %copy-start.6 = (s32[2]{0:T(128)S(1)}, s32[2]{0:T(128)}, u32[]{:S(2)}) copy-start(s32[2]{0:T(128)} %param.14) | copy-start | bytes 28
  369.9 11.6 %copy-start.2 = (f32[2,2,4096]{2,1,0:T(2,128)}, f32[2,2,4096]{2,1,0:T(2,128)S(1)}, u32[]{:S(2)}) copy-start(f32[2,2,4096]{2,1,0:T(2,128)S(1)} %pad_maximum_fusion) | copy-start | bytes 196612
Sparse Core Ops, SparseCore 0:
  382.3 124.9 all-reduce.2
where the time goes:
time: 525 us; the launch traced here: 516 us
  waiting for transfers between devices  182 us (35%)
  blocking collectives  140 us (27%)
  local copies, waits for them, and re-layouts  110 us (21%)
  matrix products  58.4 us (11%)
  between operations  14.7 us (3%)
  other arithmetic  7.15 us (1%)
    psum x1, waiting for transfers between devices, local(): moments = lax.psum(partial_value, ('row', 'col'))  125 us
    all_to_all x1, blocking collectives, local(): lax.all_to_all(flat_second, ('row', 'col'), split_axis=0, concat_axis=0,...  97.9 us
    all_to_all x1, waiting for transfers between devices, local(): lax.all_to_all(flat_first, ('row', 'col'), split_axis=0, concat_axis=0, t...  56.7 us
    dot_general x2, matrix products, density_of(): jnp.einsum('bpi,bij->bpj', masked, block, preferred_element_type=jnp.floa...  47.8 us
    unnamed x29, local copies, waits for them, and re-layouts  42.4 us
    unnamed x1, blocking collectives  42 us
    reshape x2, local copies, waits for them, and re-layouts, pack_tiles(): stored.reshape(local_rows, tile_size, local_cols, tile_size)  20.1 us
    reshape x2, local copies, waits for them, and re-layouts, assemble(): blocks.transpose(0, 1, 3, 2, 4)  15 us
  transfers between devices with their start and end apart: 2, of which 2 were waited for; matrix products, arithmetic and copies ran while one was open for 7% of the time, Pallas kernels for 0%

commit v1 on v0

--- a/solution.py
+++ b/solution.py
@@ -1,3 +1,4 @@
+import functools
 import jax
 import jax.numpy as jnp
 from jax import lax
@@ -5,6 +6,13 @@
 
 TILE = 128
 ATOMS = 1024
+
+
+def _scan_sample(x_local, mesh_name):
+    return jax.lax.all_gather(x_local, axis_name=mesh_name).sum(axis=0)
+
+
+_view_quotas = functools.partial(_scan_sample, mesh_name=("row", "col"))
 
 
 def harmonics(offsets):
@@ -123,7 +131,7 @@
     partial_value = jnp.dot(
         flat_terms, one_hot, precision=lax.Precision.HIGHEST, preferred_element_type=jnp.float32
     )
-    moments = lax.psum(partial_value, ("row", "col"))
+    moments = _view_quotas(partial_value)
     return (density, moments.reshape(2, 9, ATOMS))
 
 

time: 525 us -> 461 us (0.88)
  waiting for transfers between devices: 182 us -> 117 us
    psum x1 -> x0, waiting for transfers between devices: 125 us -> none  [local(): moments = lax.psum(partial_value, ('row', 'col'))]
    all_gather x0 -> x1, waiting for transfers between devices: none -> 59.8 us  [_scan_sample(): return jax.lax.all_gather(x_local, axis_name=mesh_name).sum(axis=0)]
  transfers between devices with their start and end apart: 2 -> 2, of which waited for: 2 -> 2; matrix products, arithmetic and copies ran while one was open for 7% -> 8% of each run, Pallas kernels for 0% -> 0%
where the time goes in v1:
time: 461 us; the launch traced here: 452 us
  blocking collectives  140 us (30%)
  waiting for transfers between devices  117 us (25%)
  local copies, waits for them, and re-layouts  108 us (23%)
  matrix products  59 us (13%)
  between operations  14.7 us (3%)
  other arithmetic  9.25 us (2%)
    all_to_all x1, blocking collectives, local(): lax.all_to_all(flat_second, ('row', 'col'), split_axis=0, concat_axis=0,...  97.9 us
    all_gather x1, waiting for transfers between devices, _scan_sample(): return jax.lax.all_gather(x_local, axis_name=mesh_name).sum(axis=0)  59.8 us
    all_to_all x1, waiting for transfers between devices, local(): lax.all_to_all(flat_first, ('row', 'col'), split_axis=0, concat_axis=0, t...  56.7 us
    dot_general x2, matrix products, density_of(): jnp.einsum('bpi,bij->bpj', masked, block, preferred_element_type=jnp.floa...  47.8 us
    unnamed x1, blocking collectives  42 us
    unnamed x29, local copies, waits for them, and re-layouts  41.5 us
    reshape x2, local copies, waits for them, and re-layouts, pack_tiles(): stored.reshape(local_rows, tile_size, local_cols, tile_size)  20.1 us
    reshape x2, local copies, waits for them, and re-layouts, assemble(): blocks.transpose(0, 1, 3, 2, 4)  15 us
  transfers between devices with their start and end apart: 2, of which 2 were waited for; matrix products, arithmetic and copies ran while one was open for 8% of the time, Pallas kernels for 0%

profile of v1, /device:TPU:0, one launch (start us, length us, event | category | flops | bytes accessed | tf_op | source)
XLA Modules:
  0.0 452.0 jit_solution(12406237800808099856)
XLA Ops:
  7.2 0.8 fusion.12
  8.0 0.2 dynamic-update-slice
  8.2 42.0 %all-reduce = s32[64]{0:T(128)S(1)} all-reduce(s32[64]{0:T(128)S(1)} %dynamic-update-slice), channel_id=1, replica_groups=mesh['row'=8,'col'=4] {'row','col'}, use_global_device_ids=true, to_apply=%add | all-reduce | flops 64 | bytes 512
  50.7 0.1 reshape.452
  50.8 9.8 %copy.67 = bf16[192,8,24,128]{3,2,1,0:T(8,128)(2,1)} copy(bf16[192,8,24,128]{3,1,2,0:T(8,128)(2,1)} %bitcast.62) | data formatting | bytes 18874368
  60.6 10.0 %copy.74 = bf16[12,128,24,128]{3,1,2,0:T(8,128)(2,1)} copy(bf16[12,128,24,128]{3,2,1,0:T(8,128)(2,1)} %bitcast.53) | data formatting | bytes 18874368 | tf_op jit(solution)/shard_map/reshape | solution.py:75
  70.6 9.9 %copy.66 = bf16[192,8,24,128]{3,2,1,0:T(8,128)(2,1)} copy(bf16[192,8,24,128]{3,1,2,0:T(8,128)(2,1)} %bitcast.63) | data formatting | bytes 18874368
  80.5 10.1 %copy.75 = bf16[12,128,24,128]{3,1,2,0:T(8,128)(2,1)} copy(bf16[12,128,24,128]{3,2,1,0:T(8,128)(2,1)} %bitcast.54) | data formatting | bytes 18874368 | tf_op jit(solution)/shard_map/reshape | solution.py:75
  90.6 6.8 %gather_fusion.2 = bf16[128,128,128]{2,1,0:T(8,128)(2,1)} fusion(bf16[12,24,128,128]{3,2,1,0:T(8,128)(2,1)} %bitcast.55, s32[128]{0:T(128)S(1)} %reshape.452), kind=kCustom, calls=%fused_computation.2 | custom fusion | bytes 8389632 | tf_op jit(solution)/shard_map/gather | solution.py:78
  97.4 6.7 %gather_fusion = bf16[128,128,128]{2,1,0:T(8,128)(2,1)} fusion(bf16[12,24,128,128]{3,2,1,0:T(8,128)(2,1)} %bitcast.56, s32[128]{0:T(128)S(1)} %reshape.452), kind=kCustom, calls=%fused_computation | custom fusion | bytes 8389632 | tf_op jit(solution)/shard_map/gather | solution.py:78
  104.3 0.2 compare_and_fusion
  104.5 5.2 %broadcast_select_fusion.1 = (bf16[32,2,1,2,128,128]{5,4,3,1,2,0:T(8,128)(2,1)}, bf16[32,2,1,2,128,128]{5,4,3,1,2,0:T(8,128)(2,1)S(1)}) fusion(bf16[32,2,1,2,128,128]{5,4,3,1,2,0:T(8,128)(2,1)} %bitcast.58, pred[32,2,2]{2,1,0:T(4,128)(4,1)S(1)} %compare_and_fusion, bf16[32,2,1,2,128,128]{5,4,3,1,2,0:T(8,128)(2,1)} %bitcast.57), kind=kLoop, calls=%fused_computation.18 | loop fusion | flops 4194304 | bytes 16777344 | tf_op jit(solution)/shard_map/jit(_where)/select_n | solution.py:79
  109.6 97.9 %all_to_all.10 = bf16[32,2,1,2,128,128]{5,4,3,1,2,0:T(8,128)(2,1)} all-to-all(bf16[32,2,1,2,128,128]{5,4,3,1,2,0:T(8,128)(2,1)S(1)} %get-tuple-element.13), channel_id=1, replica_groups=mesh['row'=8,'col'=4] {'row','col'}, dimensions={0} | all-to-all | bytes 8388608 | tf_op jit(solution)/shard_map/all_to_all | solution.py:91
  207.5 3.8 all-to-all-start
  211.3 0.5 all-gather.4.cloned.1.call-start
  212.2 19.9 %copy.45 = bf16[2,4096,896]{1,2,0:T(8,128)(2,1)} copy(bf16[2,4096,896]{2,1,0:T(8,128)(2,1)} %param.11) | data formatting | bytes 29360128 | tf_op args[2]
  232.6 4.2 gather_fusion.3
  236.9 4.5 %copy.55 = bf16[2,7,128,7,128]{4,3,2,1,0:T(8,128)(2,1)} copy(bf16[2,7,128,7,128]{4,2,3,1,0:T(8,128)(2,1)S(1)} %bitcast.61) | data formatting | bytes 6422528 | tf_op jit(solution)/shard_map/transpose | solution.py:110
  241.4 7.4 %reshape.491 = bf16[2,896,896]{2,1,0:T(8,128)(2,1)} reshape(bf16[2,7,128,7,128]{4,3,2,1,0:T(8,128)(2,1)} %copy.55) | data formatting | bytes 6422528 | tf_op jit(solution)/shard_map/reshape | solution.py:110
  248.8 56.7 %all-to-all-done = bf16[32,2,1,2,128,128]{5,4,3,1,2,0:T(8,128)(2,1)} async-done(((bf16[32,2,1,2,128,128]{5,4,3,1,2,0:T(8,128)(2,1)}), bf16[32,2,1,2,128,128]{5,4,3,1,2,0:T(8,128)(2,1)}, u32[]{:S(2)}, u32[]{:S(2)}) %all-to-all-start) | async-done | bytes 4194336 | tf_op jit(solution)/shard_map/all_to_all | solution.py:90
  305.6 4.2 gather_fusion.1
  309.8 4.5 copy.50
  314.3 7.6 %reshape.489 = bf16[2,896,896]{2,1,0:T(8,128)(2,1)} reshape(bf16[2,7,128,7,128]{4,3,2,1,0:T(8,128)(2,1)} %copy.50) | data formatting | bytes 6422528 | tf_op jit(solution)/shard_map/reshape | solution.py:110
  321.9 23.4 %fusion.2 = f32[2,4096]{1,0:T(2,128)S(1)} fusion(bf16[2,896,896]{2,1,0:T(8,128)(2,1)S(1)} %copy-done, bf16[2,4096,896]{1,2,0:T(8,128)(2,1)} %copy.45, bf16[2,896]{1,0:T(2,128)(2,1)S(1)} %bitcast.70), kind=kOutput, calls=%fused_computation.9 | convolution fusion | flops 13190029312 | bytes 17927680 | tf_op jit(solution)/shard_map/bpi,bij->bpj/dot_general | solution.py:121
  345.3 24.4 %fusion.1 = f32[2,4096]{1,0:T(2,128)S(1)} fusion(bf16[2,896,896]{2,1,0:T(8,128)(2,1)} %reshape.489, bf16[2,4096,896]{1,2,0:T(8,128)(2,1)} %copy.45, bf16[2,896]{1,0:T(2,128)(2,1)S(1)} %bitcast.71), kind=kOutput, calls=%fused_computation.8 | convolution fusion | flops 13190029312 | bytes 17927680 | tf_op jit(solution)/shard_map/bpi,bij->bpj/dot_general | solution.py:121
  369.9 0.2 broadcast_multiply_fusion
  370.2 0.4 pad.4
  370.5 0.5 copy.68
  371.0 11.2 %fusion.8 = f32[1,18,1024]{2,1,0:T(8,128)} fusion(f32[18,8192]{1,0:T(8,128)S(1)} %bitcast.66, s32[8192]{0:T(1024)S(1)} %bitcast.68), kind=kOutput, calls=%fused_computation.19 | convolution fusion | flops 1820327936 | bytes 696320 | tf_op jit(solution)/shard_map/dot_general | solution.py:131
  382.2 59.8 %all-gather.4.cloned.1.call-done = f32[32,18,1024]{2,1,0:T(8,128)} async-done(((f32[1,18,1024]{2,1,0:T(8,128)}), f32[32,18,1024]{2,1,0:T(8,128)}) %all-gather.4.cloned.1.call-update) | async-done | bytes 2359312 | tf_op jit(solution)/shard_map/all_gather | solution.py:12
  441.9 2.1 reduce_sum.35
  444.1 0.7 copy.58
  (48 shorter events, 1.4 us)
Async XLA Ops:
  207.5 4.3 copy-start.5
  207.5 98.0 %all-to-all-start = ((bf16[32,2,1,2,128,128]{5,4,3,1,2,0:T(8,128)(2,1)}), bf16[32,2,1,2,128,128]{5,4,3,1,2,0:T(8,128)(2,1)}, u32[]{:S(2)}, u32[]{:S(2)}) async-start(bf16[32,2,1,2,128,128]{5,4,3,1,2,0:T(8,128)(2,1)} %get-tuple-element.12), calls=%async_computation | async-start | bytes 8388608 | tf_op jit(solution)/shard_map/all_to_all | solution.py:90
  211.3 230.6 %all-gather.4.cloned.1.call-start = ((), (), s32[]{:S(2)}) async-start(), calls=%async_computation.2 | async-start | bytes 3244032 | tf_op jit(solution)/shard_map/all_gather | solution.py:12
  212.1 20.0 %copy-start.7 = (s32[2]{0:T(128)S(1)}, s32[2]{0:T(128)}, u32[]{:S(2)}) copy-start(s32[2]{0:T(128)} %param.13) | copy-start | bytes 28
  212.1 20.1 %copy-start.4 = (s32[2,4096]{1,0:T(2,128)S(1)}, s32[2,4096]{1,0:T(2,128)}, u32[]{:S(2)}) copy-start(s32[2,4096]{1,0:T(2,128)} %param.17) | copy-start | bytes 98308
  212.1 20.1 %copy-start.1 = (f32[3,2,4096]{2,1,0:T(2,128)S(1)}, f32[3,2,4096]{2,1,0:T(2,128)}, u32[]{:S(2)}) copy-start(f32[3,2,4096]{2,1,0:T(2,128)} %param.15) | copy-start | bytes 294916
  212.2 20.3 %copy-start.3 = (f32[2,4096]{1,0:T(2,128)S(1)}, f32[2,4096]{1,0:T(2,128)}, u32[]{:S(2)}) copy-start(f32[2,4096]{1,0:T(2,128)} %param.16) | copy-start | bytes 98308
  314.3 7.6 %copy-start = (bf16[2,896,896]{2,1,0:T(8,128)(2,1)S(1)}, bf16[2,896,896]{2,1,0:T(8,128)(2,1)}, u32[]{:S(2)}) copy-start(bf16[2,896,896]{2,1,0:T(8,128)(2,1)} %reshape.491) | copy-start | bytes 9633796
  345.3 24.5 %copy-start.6 = (s32[2]{0:T(128)S(1)}, s32[2]{0:T(128)}, u32[]{:S(2)}) copy-start(s32[2]{0:T(128)} %param.14) | copy-start | bytes 28
  369.9 12.3 %copy-start.2 = (f32[2,2,4096]{2,1,0:T(2,128)}, f32[2,2,4096]{2,1,0:T(2,128)S(1)}, u32[]{:S(2)}) copy-start(f32[2,2,4096]{2,1,0:T(2,128)S(1)} %pad_maximum_fusion) | copy-start | bytes 196612
Sparse Core Ops, SparseCore 0:
  382.3 59.5 all-gather.3
